TPU v7x, 32 devices: a whole 2x2x4 slice. The times are simulated.
32 devices in a mesh: wide: 8 (over y, x, core), narrow: 4 (over z).
Axes of the slice: x: 2, y: 2, z: 4, core: 2. Of those that a mesh axis runs over, the one named last changes fastest.
Arguments:
- measures: float32 [2, 48, 262144], P(None, 'narrow', 'wide'), may hold values from 0.1 to 10
- sku_brand: int32 [262144], P('wide'), may hold values from 0 to 8191, as said below
- sku_count: int32 [8], P('wide'), may hold values from 1024 to 32768, as said below
- brand_slot: int32 [8192], replicated, may hold values from 0 to 8191, as said below
- brand_category: int32 [8192], replicated, may hold values from 0 to 499
Outputs:
- brand_index: float32 [2, 48, 8192], P(None, 'narrow', 'wide')
- category_index: float32 [2, 48, 500], P(None, 'narrow')
Inputs may be any that keep to these rules, and one draw needn't show every extreme that they name: `sku_count`: the largest count is 32768 in every draw; the others are skewed below it. brand_slot is a permutation; columns k * 1024 to (k + 1) * 1024 - 1 form the k-th owner block. `sku_brand`: in every tile, slots o * 128 to (o + 1) * 128 - 1 name 128 distinct brands whose columns lie in owner block o, for every owner block o; every later slot of the tile names one of these brands; every brand is named by some live SKU.
All inputs are finite; a program needn't handle non-finite values.
Results may differ from a plain program's by a relative error of at most 0.002.
Values sent between devices are 32-bit elements; how exact they have to be, the bound alone decides.
A program may use at most 64 MiB of HBM per device.

v0:
```python
import math
import jax
import jax.numpy as jnp
from jax import lax
from jax.sharding import PartitionSpec as P

WEEKS = 48
CATS = 500
CAP = 128


def body(measures, sku_brand, sku_count, brand_slot, brand_category):
    kinds_here, weeks_local, tile_size = measures.shape
    measure_rows = kinds_here * weeks_local
    flat = measures.reshape(measure_rows, tile_size)
    wide_size = lax.axis_size("wide")
    brand_total = brand_slot.shape[0]
    owned_width = brand_total // wide_size
    list_count = wide_size * CAP
    live_count = sku_count[0]
    list_brands = sku_brand[:list_count]
    own_index = lax.axis_index("wide")
    own_columns = own_index * owned_width + jnp.arange(owned_width, dtype=jnp.int32)
    category_ids = jnp.arange(CATS, dtype=jnp.int32)
    brand_block = math.gcd(1024, brand_total)
    brand_trips = brand_total // brand_block

    def lookup(block_index, carry):
        list_columns, my_category, category_size = carry
        offset = block_index * brand_block
        block_slots = lax.dynamic_slice_in_dim(brand_slot, offset, brand_block, 0)
        block_cats = lax.dynamic_slice_in_dim(brand_category, offset, brand_block, 0)
        block_ids = offset + jnp.arange(brand_block, dtype=jnp.int32)
        list_columns = list_columns + jnp.sum(
            jnp.where(list_brands[:, None] == block_ids[None, :], block_slots[None, :], 0), axis=1
        )
        my_category = my_category + jnp.sum(
            jnp.where(own_columns[:, None] == block_slots[None, :], block_cats[None, :], 0), axis=1
        )
        category_size = category_size + jnp.sum(
            (block_cats[:, None] == category_ids[None, :]).astype(jnp.float32), axis=0
        )
        return (list_columns, my_category, category_size)

    start_lookup = (
        jnp.zeros((list_count,), jnp.int32),
        jnp.zeros((owned_width,), jnp.int32),
        jnp.zeros((CATS,), jnp.float32),
    )
    list_columns, my_category, category_size = lax.fori_loop(0, brand_trips, lookup, start_lookup)
    high_part = flat.astype(jnp.bfloat16)
    first_rest = flat - high_part.astype(jnp.float32)
    middle_part = first_rest.astype(jnp.bfloat16)
    low_part = (first_rest - middle_part.astype(jnp.float32)).astype(jnp.bfloat16)
    stacked = jnp.concatenate([high_part, middle_part, low_part], axis=0)
    block_size = math.gcd(2048, tile_size)
    block_trips = (live_count + block_size - 1) // block_size

    def accumulate(block_index, totals):
        offset = block_index * block_size
        values = lax.dynamic_slice_in_dim(stacked, offset, block_size, 1)
        target = lax.dynamic_slice_in_dim(sku_brand, offset, block_size, 0)
        is_live = offset + jnp.arange(block_size, dtype=jnp.int32) < live_count
        values = jnp.where(is_live[None, :], values, jnp.zeros((), jnp.bfloat16))
        member_table = (target[:, None] == list_brands[None, :]).astype(jnp.bfloat16)
        return totals + jnp.dot(values, member_table, preferred_element_type=jnp.float32)

    start_sums = jnp.zeros((3 * measure_rows, list_count), jnp.float32)
    summed = lax.fori_loop(0, block_trips, accumulate, start_sums)
    compact = (
        summed[:measure_rows] + summed[measure_rows : 2 * measure_rows] + summed[2 * measure_rows :]
    )
    local_labels = (list_columns % owned_width).reshape(wide_size, CAP)
    packed = compact.reshape(measure_rows, wide_size, CAP).transpose(1, 0, 2)
    labels = local_labels.astype(jnp.float32)
    arrived, arrived_ids = (
        lax.all_to_all(packed, "wide", split_axis=0, concat_axis=0, tiled=True),
        lax.all_to_all(labels, "wide", split_axis=0, concat_axis=0, tiled=True),
    )
    flat_ids = arrived_ids.reshape(-1).astype(jnp.int32)
    flat_values = arrived.transpose(1, 0, 2).reshape(measure_rows, -1)
    placing = (flat_ids[:, None] == jnp.arange(owned_width, dtype=jnp.int32)[None, :]).astype(
        jnp.float32
    )
    owned_sums = jnp.dot(
        flat_values, placing, precision=lax.Precision.HIGHEST, preferred_element_type=jnp.float32
    )
    membership = (my_category[:, None] == category_ids[None, :]).astype(jnp.float32)
    category_part = jnp.dot(
        owned_sums, membership, precision=lax.Precision.HIGHEST, preferred_element_type=jnp.float32
    )
    category_sums = lax.psum(category_part, "wide")
    brand_category_sum = jnp.dot(
        category_sums,
        membership.T,
        precision=lax.Precision.HIGHEST,
        preferred_element_type=jnp.float32,
    )
    brand_peers = jnp.dot(
        membership,
        category_size,
        precision=lax.Precision.HIGHEST,
        preferred_element_type=jnp.float32,
    )
    brand_index = owned_sums * brand_peers[None, :] / brand_category_sum
    by_kind = category_sums.reshape(kinds_here, weeks_local, CATS)
    kind_totals = jnp.sum(by_kind, axis=(1, 2))
    grand_sum = lax.psum(kind_totals, "narrow") / WEEKS
    category_index = by_kind * CATS / grand_sum[:, None, None]
    return (brand_index.reshape(kinds_here, weeks_local, owned_width), category_index)


def solution(mesh):
    placed = (P(None, "narrow", "wide"), P("wide"), P("wide"), P(), P())
    return jax.shard_map(
        body,
        mesh=mesh,
        in_specs=placed,
        out_specs=(P(None, "narrow", "wide"), P(None, "narrow", None)),
        check_vma=False,
    )
```

profile of v0, /device:TPU:0, one launch (start us, length us, event | category | flops | bytes accessed | tf_op | source)
XLA Modules:
  0.0 159.0 jit_solution(1127724570599743675)
XLA Ops:
  0.7 0.7 slice.12
  1.4 23.3 %while.29 = (s32[]{:T(128)}, s32[1024]{0:T(1024)S(1)}, s32[1024]{0:T(1024)S(1)}, f32[500]{0:T(512)S(1)}, s32[1024]{0:T(1024)S(1)}, /*index=5*/s32[8192]{0:T(1024...) while((s32[]{:T(128)}, s32[1024]{0:T(1024)S(1)}, ...), condition=%wide.region_6.7_spmd.clone, body=%wide.region_2.6_spmd.clone.sunk | while | flops 7832059 | bytes 90110 | solution.py:50
  2.7 1.2 select_reduce_fusion.3
  4.3 0.7 dynamic_slice.32
  5.7 1.2 select_reduce_fusion.3
  7.2 0.7 dynamic_slice.32
  8.6 1.2 select_reduce_fusion.3
  10.1 0.7 dynamic_slice.32
  11.5 1.2 select_reduce_fusion.3
  13.0 0.7 dynamic_slice.32
  14.4 1.2 select_reduce_fusion.3
  15.9 0.7 dynamic_slice.32
  17.3 1.2 select_reduce_fusion.3
  18.8 0.7 dynamic_slice.32
  20.2 1.2 select_reduce_fusion.3
  21.8 0.7 dynamic_slice.32
  23.2 1.2 select_reduce_fusion.3
  25.3 5.2 %all-to-all-start.1 = ((f32[8,1,128]{2,1,0:T(1,128)}), f32[8,1,128]{2,1,0:T(1,128)S(1)}, u32[]{:S(2)}, u32[]{:S(2)}) async-start(f32[8,1,128]{2,1,0:T(1,128)} %bitcast.3), calls=%async_computation.1 | async-start | bytes 8192 | tf_op jit(solution)/shard_map/all_to_all | solution.py:78
  31.1 5.6 %copy.21 = f32[2,12,32768]{2,1,0:T(8,128)} copy(f32[2,12,32768]{2,0,1:T(2,128)} %param.9) | data formatting | bytes 6291456 | tf_op args[0]
  36.8 2.6 %reshape.62 = f32[24,32768]{1,0:T(8,128)S(1)} reshape(f32[2,12,32768]{2,1,0:T(8,128)} %copy.21) | data formatting | bytes 6291456 | tf_op jit(solution)/shard_map/reshape | solution.py:15
  39.3 2.5 %fusion.31 = (bf16[24,32768]{1,0:T(8,128)(2,1)}, bf16[24,32768]{1,0:T(8,128)(2,1)}, bf16[24,32768]{1,0:T(8,128)(2,1)}) fusion(f32[24,32768]{1,0:T(8,128)S(1)} %reshape.62), kind=kLoop, calls=%fused_computation.49 | loop fusion | flops 5505024 | bytes 7864320 | tf_op jit(solution)/shard_map/convert_element_type | solution.py:51
  41.8 3.9 %pad_maximum_fusion = bf16[72,32768]{1,0:T(8,128)(2,1)} fusion(bf16[24,32768]{1,0:T(8,128)(2,1)} %get-tuple-element.277, bf16[24,32768]{1,0:T(8,128)(2,1)} %get-tuple-element.278, bf16[24,32768]{1,0:T(8,128)(2,1)} %get-tuple-element.276), kind=kLoop, calls=%fused_computation.23 | loop fusion | flops 14155776 | bytes 9437184 | tf_op jit(solution)/shard_map/concatenate | solution.py:55
  45.7 32.1 %while.28 = (s32[]{:T(128)}, f32[72,1024]{1,0:T(8,128)S(1)}, s32[]{:T(128)}, s32[]{:T(128)}, bf16[72,32768]{1,0:T(8,128)(2,1)}, /*index=5*/s32[32768]{0:T(1024)}...) while((s32[]{:T(128)}, f32[72,1024]{1,0:T(8,128)S(1)}, s32[]{:T(128)}, ...), condition=%wide.region_1.0_spmd, body=%wide.region_0.1_spmd.sunk | while | flops 304312320 | bytes 917675 | solution.py:69
  45.8 0.7 dynamic_slice.31
  47.1 2.6 %fusion.42 = f32[72,1024]{1,0:T(8,128)S(1)} fusion(f32[72,1024]{1,0:T(8,128)S(1)} %get-tuple-element.430, s32[1024]{0:T(1024)S(1)} %get-tuple-element.446, s32[2048]{0:T(1024)S(1)} %dynamic_slice.31, bf16[72,32768]{1,0:T(8,128)(2,1)} %get-tuple-element.444, s32[]{:T(128)S(6)} %select_n.59, pred[2048]{0:T(1024)(128)(4,1)S(1)} %add_compare_fusion.2), kind=kOutput, calls=%fused_computation.6.clone.1 | convolution fusion | flops 304308224 | bytes 899076 | tf_op jit(solution)/shard_map/while/body/dot_general | solution.py:66
  49.8 0.7 dynamic_slice.31
  51.1 2.6 %fusion.42 = f32[72,1024]{1,0:T(8,128)S(1)} fusion(f32[72,1024]{1,0:T(8,128)S(1)} %get-tuple-element.430, s32[1024]{0:T(1024)S(1)} %get-tuple-element.446, s32[2048]{0:T(1024)S(1)} %dynamic_slice.31, bf16[72,32768]{1,0:T(8,128)(2,1)} %get-tuple-element.444, s32[]{:T(128)S(6)} %select_n.59, pred[2048]{0:T(1024)(128)(4,1)S(1)} %add_compare_fusion.2), kind=kOutput, calls=%fused_computation.6.clone.1 | convolution fusion | flops 304308224 | bytes 899076 | tf_op jit(solution)/shard_map/while/body/dot_general | solution.py:66
  53.8 0.7 dynamic_slice.31
  55.2 2.6 %fusion.42 = f32[72,1024]{1,0:T(8,128)S(1)} fusion(f32[72,1024]{1,0:T(8,128)S(1)} %get-tuple-element.430, s32[1024]{0:T(1024)S(1)} %get-tuple-element.446, s32[2048]{0:T(1024)S(1)} %dynamic_slice.31, bf16[72,32768]{1,0:T(8,128)(2,1)} %get-tuple-element.444, s32[]{:T(128)S(6)} %select_n.59, pred[2048]{0:T(1024)(128)(4,1)S(1)} %add_compare_fusion.2), kind=kOutput, calls=%fused_computation.6.clone.1 | convolution fusion | flops 304308224 | bytes 899076 | tf_op jit(solution)/shard_map/while/body/dot_general | solution.py:66
  57.8 0.7 dynamic_slice.31
  59.2 2.6 %fusion.42 = f32[72,1024]{1,0:T(8,128)S(1)} fusion(f32[72,1024]{1,0:T(8,128)S(1)} %get-tuple-element.430, s32[1024]{0:T(1024)S(1)} %get-tuple-element.446, s32[2048]{0:T(1024)S(1)} %dynamic_slice.31, bf16[72,32768]{1,0:T(8,128)(2,1)} %get-tuple-element.444, s32[]{:T(128)S(6)} %select_n.59, pred[2048]{0:T(1024)(128)(4,1)S(1)} %add_compare_fusion.2), kind=kOutput, calls=%fused_computation.6.clone.1 | convolution fusion | flops 304308224 | bytes 899076 | tf_op jit(solution)/shard_map/while/body/dot_general | solution.py:66
  61.8 0.7 dynamic_slice.31
  63.2 2.6 %fusion.42 = f32[72,1024]{1,0:T(8,128)S(1)} fusion(f32[72,1024]{1,0:T(8,128)S(1)} %get-tuple-element.430, s32[1024]{0:T(1024)S(1)} %get-tuple-element.446, s32[2048]{0:T(1024)S(1)} %dynamic_slice.31, bf16[72,32768]{1,0:T(8,128)(2,1)} %get-tuple-element.444, s32[]{:T(128)S(6)} %select_n.59, pred[2048]{0:T(1024)(128)(4,1)S(1)} %add_compare_fusion.2), kind=kOutput, calls=%fused_computation.6.clone.1 | convolution fusion | flops 304308224 | bytes 899076 | tf_op jit(solution)/shard_map/while/body/dot_general | solution.py:66
  65.8 0.7 dynamic_slice.31
  67.2 2.6 %fusion.42 = f32[72,1024]{1,0:T(8,128)S(1)} fusion(f32[72,1024]{1,0:T(8,128)S(1)} %get-tuple-element.430, s32[1024]{0:T(1024)S(1)} %get-tuple-element.446, s32[2048]{0:T(1024)S(1)} %dynamic_slice.31, bf16[72,32768]{1,0:T(8,128)(2,1)} %get-tuple-element.444, s32[]{:T(128)S(6)} %select_n.59, pred[2048]{0:T(1024)(128)(4,1)S(1)} %add_compare_fusion.2), kind=kOutput, calls=%fused_computation.6.clone.1 | convolution fusion | flops 304308224 | bytes 899076 | tf_op jit(solution)/shard_map/while/body/dot_general | solution.py:66
  69.9 0.7 dynamic_slice.31
  71.2 2.6 %fusion.42 = f32[72,1024]{1,0:T(8,128)S(1)} fusion(f32[72,1024]{1,0:T(8,128)S(1)} %get-tuple-element.430, s32[1024]{0:T(1024)S(1)} %get-tuple-element.446, s32[2048]{0:T(1024)S(1)} %dynamic_slice.31, bf16[72,32768]{1,0:T(8,128)(2,1)} %get-tuple-element.444, s32[]{:T(128)S(6)} %select_n.59, pred[2048]{0:T(1024)(128)(4,1)S(1)} %add_compare_fusion.2), kind=kOutput, calls=%fused_computation.6.clone.1 | convolution fusion | flops 304308224 | bytes 899076 | tf_op jit(solution)/shard_map/while/body/dot_general | solution.py:66
  73.9 0.7 dynamic_slice.31
  75.2 2.6 %fusion.42 = f32[72,1024]{1,0:T(8,128)S(1)} fusion(f32[72,1024]{1,0:T(8,128)S(1)} %get-tuple-element.430, s32[1024]{0:T(1024)S(1)} %get-tuple-element.446, s32[2048]{0:T(1024)S(1)} %dynamic_slice.31, bf16[72,32768]{1,0:T(8,128)(2,1)} %get-tuple-element.444, s32[]{:T(128)S(6)} %select_n.59, pred[2048]{0:T(1024)(128)(4,1)S(1)} %add_compare_fusion.2), kind=kOutput, calls=%fused_computation.6.clone.1 | convolution fusion | flops 304308224 | bytes 899076 | tf_op jit(solution)/shard_map/while/body/dot_general | solution.py:66
  78.6 35.1 %all-to-all-start = ((f32[8,24,128]{2,1,0:T(8,128)}), f32[8,24,128]{2,1,0:T(8,128)S(1)}, u32[]{:S(2)}, u32[]{:S(2)}) async-start(f32[8,24,128]{2,1,0:T(8,128)} %copy.22), calls=%async_computation | async-start | bytes 196608 | tf_op jit(solution)/shard_map/all_to_all | solution.py:77
  113.7 1.1 fusion.21
  114.8 4.1 %all-to-all-done = f32[8,24,128]{2,1,0:T(8,128)S(1)} async-done(((f32[8,24,128]{2,1,0:T(8,128)}), f32[8,24,128]{2,1,0:T(8,128)S(1)}, u32[]{:S(2)}, u32[]{:S(2)}) %all-to-all-start) | async-done | bytes 98336 | tf_op jit(solution)/shard_map/all_to_all | solution.py:77
  118.9 1.5 fusion.17
  120.4 0.8 fusion.20
  121.2 22.9 %psum.14 = f32[24,500]{1,0:T(8,128)S(1)} all-reduce(f32[24,500]{1,0:T(8,128)S(1)} %fusion.20), channel_id=1, replica_groups=mesh['wide'=8,'narrow'=4] {'wide'}, use_global_device_ids=true, to_apply=%region_7.8 | all-reduce | flops 12000 | bytes 96000 | tf_op jit(solution)/shard_map/psum | solution.py:92
  144.4 12.0 %psum.15 = f32[2]{0:T(128)S(1)} all-reduce(f32[2]{0:T(128)S(1)} %reduce_sum.57), channel_id=1, replica_groups=mesh['wide'=8,'narrow'=4] {'narrow'}, use_global_device_ids=true, to_apply=%region_10.11 | all-reduce | flops 2 | bytes 16 | tf_op jit(solution)/shard_map/psum | solution.py:108
  157.1 1.1 fusion.23
  158.3 0.7 copy.24
  (75 shorter events, 16.3 us)
Async XLA Ops:
  25.3 53.3 %all-to-all-start.1 = ((f32[8,1,128]{2,1,0:T(1,128)}), f32[8,1,128]{2,1,0:T(1,128)S(1)}, u32[]{:S(2)}, u32[]{:S(2)}) async-start(f32[8,1,128]{2,1,0:T(1,128)} %bitcast.3), calls=%async_computation.1 | async-start | bytes 8192 | tf_op jit(solution)/shard_map/all_to_all | solution.py:78
  78.6 40.3 %all-to-all-start = ((f32[8,24,128]{2,1,0:T(8,128)}), f32[8,24,128]{2,1,0:T(8,128)S(1)}, u32[]{:S(2)}, u32[]{:S(2)}) async-start(f32[8,24,128]{2,1,0:T(8,128)} %copy.22), calls=%async_computation | async-start | bytes 196608 | tf_op jit(solution)/shard_map/all_to_all | solution.py:77
where the time goes:
time: 161 us; the launch traced here: 159 us
  starting transfers between devices  40.3 us (25%)
  blocking collectives  34.8 us (22%)
  local copies, waits for them, and re-layouts  27.7 us (17%)
  matrix products  25.5 us (16%)
  other arithmetic  24.5 us (15%)
  waiting for transfers between devices  4.08 us (3%)
    all_to_all x1, starting transfers between devices, body(): lax.all_to_all(packed, 'wide', split_axis=0, concat_axis=0, tiled=True)  35.1 us
    psum x1, blocking collectives, body(): category_sums = lax.psum(category_part, 'wide')  22.9 us
    dot_general x8, matrix products, accumulate(): jnp.dot(values, member_table, preferred_element_type=jnp.float32)  21 us
    psum x1, blocking collectives, body(): grand_sum = lax.psum(kind_totals, 'narrow') / WEEKS  12 us
    reduce_sum x8, other arithmetic, lookup(): jnp.sum(jnp.where(own_columns[:, None] == block_slots[None, :], block_cat...  9.44 us
    unnamed x4, local copies, waits for them, and re-layouts  7.04 us
    dynamic_slice x8, local copies, waits for them, and re-layouts, accumulate(): target = lax.dynamic_slice_in_dim(sku_brand, offset, block_size, 0)  5.62 us
    dynamic_slice x8, local copies, waits for them, and re-layouts, lookup(): lax.dynamic_slice_in_dim(brand_category, offset, brand_block, 0)  5.54 us
  transfers between devices with their start and end apart: 2, of which 1 were waited for; matrix products, arithmetic and copies ran while one was open for 30% of the time, Pallas kernels for 0%

commit v1 on v0

--- a/solution.py
+++ b/solution.py
@@ -89,7 +89,7 @@
     category_part = jnp.dot(
         owned_sums, membership, precision=lax.Precision.HIGHEST, preferred_element_type=jnp.float32
     )
-    category_sums = lax.psum(category_part, "wide")
+    category_sums = jnp.sum(lax.all_gather(category_part, "wide"), axis=0)
     brand_category_sum = jnp.dot(
         category_sums,
         membership.T,

time: 161 us -> 147 us (0.913)
  blocking collectives: 34.8 us -> 20.7 us
    psum x1 -> x0, blocking collectives: 22.9 us -> none  [body(): category_sums = lax.psum(category_part, 'wide')]
    all_gather x0 -> x1, blocking collectives: none -> 8.71 us  [body(): category_sums = jnp.sum(lax.all_gather(category_part, 'wide'), axis=0)]
  transfers between devices with their start and end apart: 2 -> 2, of which waited for: 1 -> 1; matrix products, arithmetic and copies ran while one was open for 30% -> 33% of each run, Pallas kernels for 0% -> 0%
where the time goes in v1:
time: 147 us; the launch traced here: 145 us
  starting transfers between devices  40.3 us (27%)
  local copies, waits for them, and re-layouts  27.8 us (19%)
  matrix products  25.5 us (17%)
  other arithmetic  24.5 us (17%)
  blocking collectives  20.7 us (14%)
  waiting for transfers between devices  4.08 us (3%)
    all_to_all x1, starting transfers between devices, body(): lax.all_to_all(packed, 'wide', split_axis=0, concat_axis=0, tiled=True)  35.1 us
    dot_general x8, matrix products, accumulate(): jnp.dot(values, member_table, preferred_element_type=jnp.float32)  21 us
    psum x1, blocking collectives, body(): grand_sum = lax.psum(kind_totals, 'narrow') / WEEKS  12 us
    reduce_sum x8, other arithmetic, lookup(): jnp.sum(jnp.where(own_columns[:, None] == block_slots[None, :], block_cat...  9.44 us
    all_gather x1, blocking collectives, body(): category_sums = jnp.sum(lax.all_gather(category_part, 'wide'), axis=0)  8.71 us
    unnamed x4, local copies, waits for them, and re-layouts  7.04 us
    dynamic_slice x8, local copies, waits for them, and re-layouts, accumulate(): target = lax.dynamic_slice_in_dim(sku_brand, offset, block_size, 0)  5.62 us
    dynamic_slice x8, local copies, waits for them, and re-layouts, lookup(): lax.dynamic_slice_in_dim(brand_category, offset, brand_block, 0)  5.54 us
  transfers between devices with their start and end apart: 2, of which 1 were waited for; matrix products, arithmetic and copies ran while one was open for 33% of the time, Pallas kernels for 0%

profile of v1, /device:TPU:0, one launch (start us, length us, event | category | flops | bytes accessed | tf_op | source)
XLA Modules:
  0.0 145.0 jit_solution(16472053813028527784)
XLA Ops:
  0.7 0.7 slice.12
  1.4 23.3 %while.29 = (s32[]{:T(128)}, s32[1024]{0:T(1024)S(1)}, s32[1024]{0:T(1024)S(1)}, f32[500]{0:T(512)S(1)}, s32[1024]{0:T(1024)S(1)}, /*index=5*/s32[8192]{0:T(1024...) while((s32[]{:T(128)}, s32[1024]{0:T(1024)S(1)}, ...), condition=%wide.region_6.7_spmd.clone, body=%wide.region_2.6_spmd.clone.sunk | while | flops 7832059 | bytes 90110 | solution.py:50
  2.7 1.2 select_reduce_fusion.3
  4.3 0.7 dynamic_slice.32
  5.7 1.2 select_reduce_fusion.3
  7.2 0.7 dynamic_slice.32
  8.6 1.2 select_reduce_fusion.3
  10.1 0.7 dynamic_slice.32
  11.5 1.2 select_reduce_fusion.3
  13.0 0.7 dynamic_slice.32
  14.4 1.2 select_reduce_fusion.3
  15.9 0.7 dynamic_slice.32
  17.3 1.2 select_reduce_fusion.3
  18.8 0.7 dynamic_slice.32
  20.2 1.2 select_reduce_fusion.3
  21.8 0.7 dynamic_slice.32
  23.2 1.2 select_reduce_fusion.3
  25.3 5.2 %all-to-all-start.1 = ((f32[8,1,128]{2,1,0:T(1,128)}), f32[8,1,128]{2,1,0:T(1,128)S(1)}, u32[]{:S(2)}, u32[]{:S(2)}) async-start(f32[8,1,128]{2,1,0:T(1,128)} %bitcast.3), calls=%async_computation.1 | async-start | bytes 8192 | tf_op jit(solution)/shard_map/all_to_all | solution.py:78
  31.1 5.6 %copy.20 = f32[2,12,32768]{2,1,0:T(8,128)} copy(f32[2,12,32768]{2,0,1:T(2,128)} %param.9) | data formatting | bytes 6291456 | tf_op args[0]
  36.8 2.6 %reshape.62 = f32[24,32768]{1,0:T(8,128)S(1)} reshape(f32[2,12,32768]{2,1,0:T(8,128)} %copy.20) | data formatting | bytes 6291456 | tf_op jit(solution)/shard_map/reshape | solution.py:15
  39.3 2.5 %fusion.31 = (bf16[24,32768]{1,0:T(8,128)(2,1)}, bf16[24,32768]{1,0:T(8,128)(2,1)}, bf16[24,32768]{1,0:T(8,128)(2,1)}) fusion(f32[24,32768]{1,0:T(8,128)S(1)} %reshape.62), kind=kLoop, calls=%fused_computation.49 | loop fusion | flops 5505024 | bytes 7864320 | tf_op jit(solution)/shard_map/convert_element_type | solution.py:51
  41.8 3.9 %pad_maximum_fusion = bf16[72,32768]{1,0:T(8,128)(2,1)} fusion(bf16[24,32768]{1,0:T(8,128)(2,1)} %get-tuple-element.277, bf16[24,32768]{1,0:T(8,128)(2,1)} %get-tuple-element.278, bf16[24,32768]{1,0:T(8,128)(2,1)} %get-tuple-element.276), kind=kLoop, calls=%fused_computation.23 | loop fusion | flops 14155776 | bytes 9437184 | tf_op jit(solution)/shard_map/concatenate | solution.py:55
  45.7 32.1 %while.28 = (s32[]{:T(128)}, f32[72,1024]{1,0:T(8,128)S(1)}, s32[]{:T(128)}, s32[]{:T(128)}, bf16[72,32768]{1,0:T(8,128)(2,1)}, /*index=5*/s32[32768]{0:T(1024)}...) while((s32[]{:T(128)}, f32[72,1024]{1,0:T(8,128)S(1)}, s32[]{:T(128)}, ...), condition=%wide.region_1.0_spmd, body=%wide.region_0.1_spmd.sunk | while | flops 304312320 | bytes 917675 | solution.py:69
  45.8 0.7 dynamic_slice.31
  47.1 2.6 %fusion.41 = f32[72,1024]{1,0:T(8,128)S(1)} fusion(f32[72,1024]{1,0:T(8,128)S(1)} %get-tuple-element.428, s32[1024]{0:T(1024)S(1)} %get-tuple-element.444, s32[2048]{0:T(1024)S(1)} %dynamic_slice.31, bf16[72,32768]{1,0:T(8,128)(2,1)} %get-tuple-element.442, s32[]{:T(128)S(6)} %select_n.59, pred[2048]{0:T(1024)(128)(4,1)S(1)} %add_compare_fusion.2), kind=kOutput, calls=%fused_computation.6.clone.1 | convolution fusion | flops 304308224 | bytes 899076 | tf_op jit(solution)/shard_map/while/body/dot_general | solution.py:66
  49.8 0.7 dynamic_slice.31
  51.1 2.6 %fusion.41 = f32[72,1024]{1,0:T(8,128)S(1)} fusion(f32[72,1024]{1,0:T(8,128)S(1)} %get-tuple-element.428, s32[1024]{0:T(1024)S(1)} %get-tuple-element.444, s32[2048]{0:T(1024)S(1)} %dynamic_slice.31, bf16[72,32768]{1,0:T(8,128)(2,1)} %get-tuple-element.442, s32[]{:T(128)S(6)} %select_n.59, pred[2048]{0:T(1024)(128)(4,1)S(1)} %add_compare_fusion.2), kind=kOutput, calls=%fused_computation.6.clone.1 | convolution fusion | flops 304308224 | bytes 899076 | tf_op jit(solution)/shard_map/while/body/dot_general | solution.py:66
  53.8 0.7 dynamic_slice.31
  55.2 2.6 %fusion.41 = f32[72,1024]{1,0:T(8,128)S(1)} fusion(f32[72,1024]{1,0:T(8,128)S(1)} %get-tuple-element.428, s32[1024]{0:T(1024)S(1)} %get-tuple-element.444, s32[2048]{0:T(1024)S(1)} %dynamic_slice.31, bf16[72,32768]{1,0:T(8,128)(2,1)} %get-tuple-element.442, s32[]{:T(128)S(6)} %select_n.59, pred[2048]{0:T(1024)(128)(4,1)S(1)} %add_compare_fusion.2), kind=kOutput, calls=%fused_computation.6.clone.1 | convolution fusion | flops 304308224 | bytes 899076 | tf_op jit(solution)/shard_map/while/body/dot_general | solution.py:66
  57.8 0.7 dynamic_slice.31
  59.2 2.6 %fusion.41 = f32[72,1024]{1,0:T(8,128)S(1)} fusion(f32[72,1024]{1,0:T(8,128)S(1)} %get-tuple-element.428, s32[1024]{0:T(1024)S(1)} %get-tuple-element.444, s32[2048]{0:T(1024)S(1)} %dynamic_slice.31, bf16[72,32768]{1,0:T(8,128)(2,1)} %get-tuple-element.442, s32[]{:T(128)S(6)} %select_n.59, pred[2048]{0:T(1024)(128)(4,1)S(1)} %add_compare_fusion.2), kind=kOutput, calls=%fused_computation.6.clone.1 | convolution fusion | flops 304308224 | bytes 899076 | tf_op jit(solution)/shard_map/while/body/dot_general | solution.py:66
  61.8 0.7 dynamic_slice.31
  63.2 2.6 %fusion.41 = f32[72,1024]{1,0:T(8,128)S(1)} fusion(f32[72,1024]{1,0:T(8,128)S(1)} %get-tuple-element.428, s32[1024]{0:T(1024)S(1)} %get-tuple-element.444, s32[2048]{0:T(1024)S(1)} %dynamic_slice.31, bf16[72,32768]{1,0:T(8,128)(2,1)} %get-tuple-element.442, s32[]{:T(128)S(6)} %select_n.59, pred[2048]{0:T(1024)(128)(4,1)S(1)} %add_compare_fusion.2), kind=kOutput, calls=%fused_computation.6.clone.1 | convolution fusion | flops 304308224 | bytes 899076 | tf_op jit(solution)/shard_map/while/body/dot_general | solution.py:66
  65.8 0.7 dynamic_slice.31
  67.2 2.6 %fusion.41 = f32[72,1024]{1,0:T(8,128)S(1)} fusion(f32[72,1024]{1,0:T(8,128)S(1)} %get-tuple-element.428, s32[1024]{0:T(1024)S(1)} %get-tuple-element.444, s32[2048]{0:T(1024)S(1)} %dynamic_slice.31, bf16[72,32768]{1,0:T(8,128)(2,1)} %get-tuple-element.442, s32[]{:T(128)S(6)} %select_n.59, pred[2048]{0:T(1024)(128)(4,1)S(1)} %add_compare_fusion.2), kind=kOutput, calls=%fused_computation.6.clone.1 | convolution fusion | flops 304308224 | bytes 899076 | tf_op jit(solution)/shard_map/while/body/dot_general | solution.py:66
  69.9 0.7 dynamic_slice.31
  71.2 2.6 %fusion.41 = f32[72,1024]{1,0:T(8,128)S(1)} fusion(f32[72,1024]{1,0:T(8,128)S(1)} %get-tuple-element.428, s32[1024]{0:T(1024)S(1)} %get-tuple-element.444, s32[2048]{0:T(1024)S(1)} %dynamic_slice.31, bf16[72,32768]{1,0:T(8,128)(2,1)} %get-tuple-element.442, s32[]{:T(128)S(6)} %select_n.59, pred[2048]{0:T(1024)(128)(4,1)S(1)} %add_compare_fusion.2), kind=kOutput, calls=%fused_computation.6.clone.1 | convolution fusion | flops 304308224 | bytes 899076 | tf_op jit(solution)/shard_map/while/body/dot_general | solution.py:66
  73.9 0.7 dynamic_slice.31
  75.2 2.6 %fusion.41 = f32[72,1024]{1,0:T(8,128)S(1)} fusion(f32[72,1024]{1,0:T(8,128)S(1)} %get-tuple-element.428, s32[1024]{0:T(1024)S(1)} %get-tuple-element.444, s32[2048]{0:T(1024)S(1)} %dynamic_slice.31, bf16[72,32768]{1,0:T(8,128)(2,1)} %get-tuple-element.442, s32[]{:T(128)S(6)} %select_n.59, pred[2048]{0:T(1024)(128)(4,1)S(1)} %add_compare_fusion.2), kind=kOutput, calls=%fused_computation.6.clone.1 | convolution fusion | flops 304308224 | bytes 899076 | tf_op jit(solution)/shard_map/while/body/dot_general | solution.py:66
  78.6 35.1 %all-to-all-start = ((f32[8,24,128]{2,1,0:T(8,128)}), f32[8,24,128]{2,1,0:T(8,128)S(1)}, u32[]{:S(2)}, u32[]{:S(2)}) async-start(f32[8,24,128]{2,1,0:T(8,128)} %copy.21), calls=%async_computation | async-start | bytes 196608 | tf_op jit(solution)/shard_map/all_to_all | solution.py:77
  113.7 1.1 fusion.21
  114.8 4.1 %all-to-all-done = f32[8,24,128]{2,1,0:T(8,128)S(1)} async-done(((f32[8,24,128]{2,1,0:T(8,128)}), f32[8,24,128]{2,1,0:T(8,128)S(1)}, u32[]{:S(2)}, u32[]{:S(2)}) %all-to-all-start) | async-done | bytes 98336 | tf_op jit(solution)/shard_map/all_to_all | solution.py:77
  118.9 1.5 %fusion.17 = f32[24,1024]{1,0:T(8,128)S(1)} fusion(s32[1024]{0:T(1024)S(1)} %bitcast.26, f32[8,24,128]{2,1,0:T(8,128)S(1)} %all-to-all-done), kind=kOutput, calls=%fused_computation.25 | convolution fusion | flops 303038464 | bytes 200704 | tf_op jit(solution)/shard_map/dot_general | solution.py:85
  120.4 0.8 fusion.20
  121.2 8.7 %all-gather = f32[192,500]{1,0:T(8,128)S(1)} all-gather(f32[24,500]{1,0:T(8,128)S(1)} %fusion.20), channel_id=2, replica_groups=mesh['wide'=8,'narrow'=4] {'wide'}, dimensions={0}, use_global_device_ids=true | all-gather | bytes 432000 | tf_op jit(solution)/shard_map/all_gather | solution.py:92
  130.4 12.0 %psum.7 = f32[2]{0:T(128)S(1)} all-reduce(f32[2]{0:T(128)S(1)} %reduce_sum.67), channel_id=1, replica_groups=mesh['wide'=8,'narrow'=4] {'narrow'}, use_global_device_ids=true, to_apply=%region_10.11 | all-reduce | flops 2 | bytes 16 | tf_op jit(solution)/shard_map/psum | solution.py:108
  143.1 1.1 fusion.23
  144.3 0.7 copy.23
  (79 shorter events, 16.5 us)
Async XLA Ops:
  25.3 53.3 %all-to-all-start.1 = ((f32[8,1,128]{2,1,0:T(1,128)}), f32[8,1,128]{2,1,0:T(1,128)S(1)}, u32[]{:S(2)}, u32[]{:S(2)}) async-start(f32[8,1,128]{2,1,0:T(1,128)} %bitcast.3), calls=%async_computation.1 | async-start | bytes 8192 | tf_op jit(solution)/shard_map/all_to_all | solution.py:78
  78.6 40.3 %all-to-all-start = ((f32[8,24,128]{2,1,0:T(8,128)}), f32[8,24,128]{2,1,0:T(8,128)S(1)}, u32[]{:S(2)}, u32[]{:S(2)}) async-start(f32[8,24,128]{2,1,0:T(8,128)} %copy.21), calls=%async_computation | async-start | bytes 196608 | tf_op jit(solution)/shard_map/all_to_all | solution.py:77
